TPU v7x, 256 devices: a whole 4x4x8 slice. The times are simulated.
256 devices in a mesh: grid: 64 (over z, x, core), band: 4 (over y).
Axes of the slice: x: 4, y: 4, z: 8, core: 2. Of those that a mesh axis runs over, the one named last changes fastest.
Arguments:
- basis: float32 [2048, 65536], P('band', 'grid'), as said below
- panel: float32 [1024, 65536], P('band', 'grid'), may hold values from -6 to 6
Outputs:
- new_panel: float32 [1024, 65536], P('band', 'grid')
- coeffs: float32 [2048, 1024], P('band')
Inputs may be any that keep to these rules, and one draw needn't show every extreme that they name: The rows of basis are orthogonal to each other, each with squared sum 65536 (to float32 rounding).
All inputs are finite; a program needn't handle non-finite values.
Results may differ from a plain program's by a relative error of at most 0.000073.
Values sent between devices are 32-bit elements; how exact they have to be, the bound alone decides.
A program may use at most 128 MiB of HBM per device.

v0:
```python
import jax
import jax.numpy as jnp
from jax import lax
from jax.sharding import PartitionSpec as P


def together(arrays, axis):
    ravelled, at, finished = (jnp.concatenate([a.reshape(-1) for a in arrays]), 0, [])
    total = lax.psum(ravelled, axis)
    for a in arrays:
        finished.append(total[at : at + a.size].reshape(a.shape))
        at += a.size
    return tuple(finished)


def cut_along(array, dim, count):
    before, after = (array.shape[:dim], array.shape[dim + 1 :])
    return jnp.moveaxis(array.reshape(*before, count, -1, *after), dim, 0)


def summed_on_arrival(array, axis, dim):
    blocks = cut_along(array, dim, lax.axis_size(axis))
    arrived = lax.all_to_all(blocks, axis, split_axis=0, concat_axis=0, tiled=True)
    return arrived.sum(axis=0)


def tdot(left, right):
    return lax.dot_general(
        left,
        right,
        (((1,), (1,)), ((), ())),
        precision=lax.Precision.HIGHEST,
        preferred_element_type=jnp.float32,
    )


def ndot(left, right):
    return jnp.dot(left, right, precision=lax.Precision.HIGHEST)


def body(basis, panel):
    n_grid = panel.shape[1] * lax.axis_size("grid")
    n_band = lax.axis_size("band")
    rows_q = basis.shape[0]
    rows_p = panel.shape[0]
    n_panel = rows_p * n_band
    stacked = jnp.concatenate([basis, panel], 0)
    both = tdot(stacked, lax.all_gather(panel, "band", axis=0, tiled=True))
    coeff_sum, gram_sum = together((both[:rows_q], both[rows_q:]), "grid")
    coeffs = coeff_sum / n_grid
    projected = panel - lax.psum_scatter(
        ndot(coeffs.T, basis), "band", scatter_dimension=0, tiled=True
    )
    gram_part = gram_sum / n_grid - summed_on_arrival(ndot(coeffs.T, coeffs), "band", 0)
    gram = lax.all_gather(gram_part, "band", axis=0, tiled=True)
    factor = jnp.linalg.cholesky(gram)
    offset = lax.axis_index("band") * rows_p
    row_ids = lax.broadcasted_iota(jnp.int32, (n_panel, rows_p), 0)
    col_ids = lax.broadcasted_iota(jnp.int32, (n_panel, rows_p), 1)
    unit_cols = (row_ids == col_ids + offset).astype(jnp.float32)
    inverse_rows = lax.linalg.triangular_solve(
        factor, unit_cols, left_side=True, lower=True, transpose_a=True
    ).T
    new_panel = ndot(inverse_rows, lax.all_gather(projected, "band", axis=0, tiled=True))
    return (new_panel, coeffs)


def solution(mesh):
    placed = (P("band", "grid"), P("band", "grid"))
    return jax.shard_map(
        body,
        mesh=mesh,
        in_specs=placed,
        out_specs=(P("band", "grid"), P("band", None)),
        check_vma=False,
    )
```

profile of v0, /device:TPU:1, one launch (start us, length us, event | category | flops | bytes accessed | tf_op | source)
XLA Modules:
  0.0 783.9 jit_solution(712397003574629770)
XLA Ops:
  7.9 56.3 %all-gather.4.cloned.1.call-done = f32[1024,1024]{1,0:T(8,128)} async-done(((f32[256,1024]{1,0:T(8,128)}), f32[1024,1024]{1,0:T(8,128)}) %all-gather.4.cloned.1.call-update) | async-done | bytes 4194320 | tf_op jit(solution)/shard_map/all_gather | solution.py:48
  64.2 12.5 %fusion.1 = f32[768,1024]{1,0:T(8,128)S(1)} fusion(f32[1024,1024]{1,0:T(8,128)} %all-gather.4.cloned.1.call-done, f32[256,1024]{1,0:T(8,128)} %param.3, f32[512,1024]{1,0:T(8,128)} %param.2), kind=kOutput, calls=%fused_computation.6 | convolution fusion | flops 9664462848 | bytes 10485760 | tf_op jit(solution)/shard_map/dot_general | solution.py:28
  79.8 191.7 %all-reduce.3.cloned.1.call-done = f32[786432]{0:T(1024)} async-done(((f32[786432]{0:T(1024)}), f32[786432]{0:T(1024)}) %all-reduce.3.cloned.1.call-update) | async-done | bytes 3145744 | tf_op jit(solution)/shard_map/psum | solution.py:9
  274.7 10.2 %fusion.69 = f32[1024,1024]{1,0:T(8,128)} fusion(f32[512,1024]{1,0:T(8,128)} %div.29, f32[512,1024]{1,0:T(8,128)} %param.2), kind=kOutput, calls=%fused_computation.169 | convolution fusion | flops 6442450944 | bytes 8388608 | tf_op jit(solution)/shard_map/dot_general | solution.py:38
  286.4 3.1 copy.13
  289.5 9.9 %fusion.68 = f32[4,256,1024]{2,1,0:T(8,128)} fusion(f32[4,256,512]{2,1,0:T(8,128)} %bitcast.110, f32[512,1024,1]{1,0,2:T(8,128)S(1)} %copy-done.2), kind=kOutput, calls=%fused_computation.168 | convolution fusion | flops 6442450944 | bytes 8388608 | tf_op jit(solution)/shard_map/dot_general | solution.py:38
  299.4 4.9 all-to-all-start
  306.2 72.1 %all-to-all-done = f32[4,256,1024]{2,1,0:T(8,128)} async-done(((f32[4,256,1024]{2,1,0:T(8,128)}), f32[4,256,1024]{2,1,0:T(8,128)}, u32[]{:S(2)}, u32[]{:S(2)}) %all-to-all-start) | async-done | bytes 4194336 | tf_op jit(solution)/shard_map/all_to_all | solution.py:23
  378.3 3.7 reduce_sum.9
  387.5 48.0 %all-gather.6.cloned.1.call-done = f32[1024,1024]{0,1:T(8,128)} async-done(((f32[256,1024]{0,1:T(8,128)}), f32[1024,1024]{0,1:T(8,128)}) %all-gather.6.cloned.1.call-update) | async-done | bytes 4194320 | tf_op jit(solution)/shard_map/all_gather | solution.py:55
  435.5 5.5 copy.12
  441.1 4.4 fusion
  447.5 11.7 %cholesky.223 = f32[128,128]{1,0:T(8,128)S(1)} custom-call(f32[128,128]{1,0:T(8,128)S(1)} %cholesky.580), custom_call_target="Cholesky" | custom-call | tf_op jit(solution)/shard_map/jit(cholesky)/cholesky | solution.py:56
  459.2 2.5 cholesky.255
  461.8 9.8 %custom-call.62 = f32[1,128,128]{1,2,0:T(8,128)S(1)} custom-call(f32[1,128,128]{2,1,0:T(8,128)S(1)} %get-tuple-element.41), custom_call_target="InvertDiagBlocksLowerTriangular" | custom-call | tf_op jit(solution)/shard_map/jit(cholesky)/cholesky | solution.py:56
  475.5 12.1 %cholesky.244 = f32[128,128]{1,0:T(8,128)S(1)} custom-call(f32[128,128]{1,0:T(8,128)S(1)} %cholesky.584), custom_call_target="Cholesky" | custom-call | tf_op jit(solution)/shard_map/jit(cholesky)/cholesky | solution.py:56
  488.2 9.8 %custom-call.63 = f32[1,128,128]{1,2,0:T(8,128)S(1)} custom-call(f32[1,128,128]{2,1,0:T(8,128)S(1)} %get-tuple-element.38), custom_call_target="InvertDiagBlocksLowerTriangular" | custom-call | tf_op jit(solution)/shard_map/jit(cholesky)/cholesky | solution.py:56
  501.4 11.7 %cholesky.468 = f32[128,128]{1,0:T(8,128)S(1)} custom-call(f32[128,128]{1,0:T(8,128)S(1)} %cholesky.589), custom_call_target="Cholesky" | custom-call | tf_op jit(solution)/shard_map/jit(cholesky)/cholesky | solution.py:56
  514.4 9.8 %custom-call.64 = f32[1,128,128]{1,2,0:T(8,128)S(1)} custom-call(f32[1,128,128]{2,1,0:T(8,128)S(1)} %get-tuple-element.35), custom_call_target="InvertDiagBlocksLowerTriangular" | custom-call | tf_op jit(solution)/shard_map/jit(cholesky)/cholesky | solution.py:56
  527.7 11.8 %cholesky.487 = f32[128,128]{1,0:T(8,128)S(1)} custom-call(f32[128,128]{1,0:T(8,128)S(1)} %cholesky.594), custom_call_target="Cholesky" | custom-call | tf_op jit(solution)/shard_map/jit(cholesky)/cholesky | solution.py:56
  540.8 9.8 %custom-call.65 = f32[1,128,128]{1,2,0:T(8,128)S(1)} custom-call(f32[1,128,128]{2,1,0:T(8,128)S(1)} %get-tuple-element.32), custom_call_target="InvertDiagBlocksLowerTriangular" | custom-call | tf_op jit(solution)/shard_map/jit(cholesky)/cholesky | solution.py:56
  554.1 11.7 %cholesky.506 = f32[128,128]{1,0:T(8,128)S(1)} custom-call(f32[128,128]{1,0:T(8,128)S(1)} %cholesky.599), custom_call_target="Cholesky" | custom-call | tf_op jit(solution)/shard_map/jit(cholesky)/cholesky | solution.py:56
  567.2 10.0 %custom-call.66 = f32[1,128,128]{1,2,0:T(8,128)S(1)} custom-call(f32[1,128,128]{2,1,0:T(8,128)S(1)} %get-tuple-element.29), custom_call_target="InvertDiagBlocksLowerTriangular" | custom-call | tf_op jit(solution)/shard_map/jit(cholesky)/cholesky | solution.py:56
  580.5 11.7 %cholesky.526 = f32[128,128]{1,0:T(8,128)S(1)} custom-call(f32[128,128]{1,0:T(8,128)S(1)} %cholesky.604), custom_call_target="Cholesky" | custom-call | tf_op jit(solution)/shard_map/jit(cholesky)/cholesky | solution.py:56
  593.4 9.8 %custom-call.67 = f32[1,128,128]{1,2,0:T(8,128)S(1)} custom-call(f32[1,128,128]{2,1,0:T(8,128)S(1)} %get-tuple-element.26), custom_call_target="InvertDiagBlocksLowerTriangular" | custom-call | tf_op jit(solution)/shard_map/jit(cholesky)/cholesky | solution.py:56
  606.2 12.1 %cholesky.546 = f32[128,128]{1,0:T(8,128)S(1)} custom-call(f32[128,128]{1,0:T(8,128)S(1)} %cholesky.609), custom_call_target="Cholesky" | custom-call | tf_op jit(solution)/shard_map/jit(cholesky)/cholesky | solution.py:56
  619.7 9.8 %custom-call.68 = f32[1,128,128]{1,2,0:T(8,128)S(1)} custom-call(f32[1,128,128]{2,1,0:T(8,128)S(1)} %get-tuple-element.23), custom_call_target="InvertDiagBlocksLowerTriangular" | custom-call | tf_op jit(solution)/shard_map/jit(cholesky)/cholesky | solution.py:56
  632.1 11.7 %cholesky.564 = f32[128,128]{1,0:T(8,128)S(1)} custom-call(f32[128,128]{1,0:T(8,128)S(1)} %convolution_subtract_fusion.13), custom_call_target="Cholesky" | custom-call | tf_op jit(solution)/shard_map/jit(cholesky)/cholesky | solution.py:56
  650.7 4.8 select_select_fusion
  655.5 22.6 %while.1 = (s32[]{:T(128)}, f32[1024,1024]{1,0:T(8,128)}, s32[8,2]{0,1:T(2,128)S(1)}, f32[8,128,128]{2,1,0:T(8,128)S(1)}, s32[]{:T(128)}) while((s32[]{:T(128)}, f32[1024,1024]{1,0:T(8,128)}, s32[8,2]{0,1:T(2,128)S(1)}, f32[8,128,128]{2,1,0:T(8,128)S(1)}, s32[]{:T(128)}) %tuple.43), condition=%wide.while_cond, body=%wide.while_body.sunk | while | flops 2 | bytes 131181 | solution.py:61
  678.1 78.8 %custom-call.69 = f32[8,128,128]{1,2,0:T(8,128)S(1)} custom-call(f32[8,128,128]{2,1,0:T(8,128)S(1)} %get-tuple-element.9), custom_call_target="InvertDiagBlocksLowerTriangular" | custom-call | tf_op jit(solution)/shard_map/triangular_solve | solution.py:61
  770.4 6.8 fusion.70
  (134 shorter events, 85.7 us)
Async XLA Ops:
  7.2 57.1 %all-gather.4.cloned.1.call-start = ((), (), s32[]{:S(2)}) async-start(), calls=%async_computation.2 | async-start | bytes 5242880 | tf_op jit(solution)/shard_map/all_gather | solution.py:48
  7.9 263.6 %all-reduce.3.cloned.1.call-start = ((), (), s32[]{:S(2)}) async-start(), calls=%async_computation.3 | async-start | bytes 6291456 | tf_op jit(solution)/shard_map/psum | solution.py:9
  79.5 305.5 %reduce-scatter.2.cloned.1.call-start = ((), (), s32[]{:S(2)}) async-start(), calls=%async_computation.5 | async-start | bytes 5242880 | tf_op jit(solution)/shard_map/reduce_scatter | solution.py:51
  286.4 3.1 copy-start.2
  299.4 78.9 %all-to-all-start = ((f32[4,256,1024]{2,1,0:T(8,128)}), f32[4,256,1024]{2,1,0:T(8,128)}, u32[]{:S(2)}, u32[]{:S(2)}) async-start(f32[4,256,1024]{2,1,0:T(8,128)} %fusion.68), calls=%async_computation | async-start | bytes 8388608 | tf_op jit(solution)/shard_map/all_to_all | solution.py:23
  304.4 131.2 %all-gather.6.cloned.1.call-start = ((), (), s32[]{:S(2)}) async-start(), calls=%async_computation.4 | async-start | bytes 5242880 | tf_op jit(solution)/shard_map/all_gather | solution.py:55
  382.0 3.1 copy-start.1
  384.7 385.7 %all-gather.8.cloned.1.call-start = ((), (), s32[]{:S(2)}) async-start(), calls=%async_computation.6 | async-start | bytes 5242880 | tf_op jit(solution)/shard_map/all_gather | solution.py:64
  445.5 2.0 copy-start
Sparse Core Ops, SparseCore 0:
  9.8 54.3 all-gather.3
  79.7 191.8 all-reduce.2
  285.1 73.5 reduce-scatter.1
  384.9 50.6 all-gather.5
  437.2 51.1 all-gather.7
where the time goes:
time: 790 us; the launch traced here: 784 us
  waiting for transfers between devices  369 us (47%)
  other arithmetic  273 us (35%)
  matrix products  75.5 us (10%)
  local copies, waits for them, and re-layouts  41.8 us (5%)
  between operations  19.4 us (2%)
    psum x1, waiting for transfers between devices, together(): total = lax.psum(ravelled, axis)  192 us
    another operation x30, other arithmetic, body(): factor = jnp.linalg.cholesky(gram)  172 us
    another operation x3, other arithmetic, body(): lax.linalg.triangular_solve(factor, unit_cols, left_side=True, lower=True...  83.6 us
    all_to_all x1, waiting for transfers between devices, summed_on_arrival(): lax.all_to_all(blocks, axis, split_axis=0, concat_axis=0, tiled=True)  72.1 us
    all_gather x1, waiting for transfers between devices, body(): both = tdot(stacked, lax.all_gather(panel, 'band', axis=0, tiled=True))  56.3 us
    all_gather x1, waiting for transfers between devices, body(): gram = lax.all_gather(gram_part, 'band', axis=0, tiled=True)  48 us
    dot_general x3, matrix products, ndot(): return jnp.dot(left, right, precision=lax.Precision.HIGHEST)  26.8 us
    another operation x14, matrix products, body(): factor = jnp.linalg.cholesky(gram)  23.1 us
  transfers between devices with their start and end apart: 6, of which 4 were waited for; matrix products, arithmetic and copies ran while one was open for 45% of the time, Pallas kernels for 0%

commit v1 on v0

--- a/solution.py
+++ b/solution.py
@@ -52,7 +52,26 @@
         ndot(coeffs.T, basis), "band", scatter_dimension=0, tiled=True
     )
     gram_part = gram_sum / n_grid - summed_on_arrival(ndot(coeffs.T, coeffs), "band", 0)
-    gram = lax.all_gather(gram_part, "band", axis=0, tiled=True)
+    size, position, rows = (lax.axis_size("band"), lax.axis_index("band"), gram_part.shape[0])
+    upward = [(i, (i + 1) % size) for i in range(size)]
+    left_2 = [(i, (i - 1) % size) for i in range(size)]
+    result = jnp.zeros(
+        (*gram_part.shape[:0], size * rows, *gram_part.shape[0 + 1 :]), gram_part.dtype
+    )
+    result = lax.dynamic_update_slice_in_dim(result, gram_part, position * rows, axis=0)
+    from_left = from_right = gram_part
+    half = size // 2
+    for step in range(1, half + 1):
+        from_left = lax.ppermute(from_left, "band", upward)
+        result = lax.dynamic_update_slice_in_dim(
+            result, from_left, (position - step) % size * rows, axis=0
+        )
+        if step < size - half:
+            from_right = lax.ppermute(from_right, "band", left_2)
+            result = lax.dynamic_update_slice_in_dim(
+                result, from_right, (position + step) % size * rows, axis=0
+            )
+    gram = result
     factor = jnp.linalg.cholesky(gram)
     offset = lax.axis_index("band") * rows_p
     row_ids = lax.broadcasted_iota(jnp.int32, (n_panel, rows_p), 0)

time: 790 us -> 802 us (1.015)
  the two profiles are of different devices: /device:TPU:1 before, /device:TPU:32 now
where the time goes in v1:
time: 802 us; the launch traced here: 793 us
  waiting for transfers between devices  359 us (45%)
  other arithmetic  267 us (33%)
  matrix products  76.6 us (10%)
  local copies, waits for them, and re-layouts  61.3 us (8%)
  between operations  19.8 us (2%)
  starting transfers between devices  8.41 us (1%)
    psum x1, waiting for transfers between devices, together(): total = lax.psum(ravelled, axis)  191 us
    another operation x30, other arithmetic, body(): factor = jnp.linalg.cholesky(gram)  167 us
    another operation x3, other arithmetic, body(): lax.linalg.triangular_solve(factor, unit_cols, left_side=True, lower=True...  84.3 us
    ppermute x2, waiting for transfers between devices, body(): from_left = lax.ppermute(from_left, 'band', upward)  63.4 us
    all_gather x1, waiting for transfers between devices, body(): both = tdot(stacked, lax.all_gather(panel, 'band', axis=0, tiled=True))  55.3 us
    all_to_all x1, waiting for transfers between devices, summed_on_arrival(): lax.all_to_all(blocks, axis, split_axis=0, concat_axis=0, tiled=True)  48.1 us
    another operation x40, local copies, waits for them, and re-layouts  28 us
    another operation x14, matrix products, body(): factor = jnp.linalg.cholesky(gram)  27.5 us
  transfers between devices with their start and end apart: 8, of which 6 were waited for; matrix products, arithmetic and copies ran while one was open for 45% of the time, Pallas kernels for 0%

profile of v1, /device:TPU:32, one launch (start us, length us, event | category | flops | bytes accessed | tf_op | source)
XLA Modules:
  0.0 793.1 jit_solution(15723654454524131206)
XLA Ops:
  7.9 55.3 %all-gather.3.cloned.1.call-done = f32[1024,1024]{1,0:T(8,128)} async-done(((f32[256,1024]{1,0:T(8,128)}), f32[1024,1024]{1,0:T(8,128)}) %all-gather.3.cloned.1.call-update) | async-done | bytes 4194320 | tf_op jit(solution)/shard_map/all_gather | solution.py:48
  63.2 12.5 %fusion.1 = f32[768,1024]{1,0:T(8,128)S(1)} fusion(f32[1024,1024]{1,0:T(8,128)} %all-gather.3.cloned.1.call-done, f32[256,1024]{1,0:T(8,128)} %param.3, f32[512,1024]{1,0:T(8,128)} %param.2), kind=kOutput, calls=%fused_computation.6 | convolution fusion | flops 9664462848 | bytes 10485760 | tf_op jit(solution)/shard_map/dot_general | solution.py:28
  78.5 191.1 %all-reduce.3.cloned.1.call-done = f32[786432]{0:T(1024)} async-done(((f32[786432]{0:T(1024)}), f32[786432]{0:T(1024)}) %all-reduce.3.cloned.1.call-update) | async-done | bytes 3145744 | tf_op jit(solution)/shard_map/psum | solution.py:9
  277.4 9.9 %fusion.85 = f32[4,256,1024]{2,1,0:T(8,128)} fusion(f32[4,256,512]{2,1,0:T(8,128)} %bitcast.108, f32[512,1024,1]{1,0,2:T(8,128)S(1)} %copy-done.4), kind=kOutput, calls=%fused_computation.179 | convolution fusion | flops 6442450944 | bytes 8388608 | tf_op jit(solution)/shard_map/dot_general | solution.py:38
  287.3 4.8 all-to-all-start
  294.2 48.1 %all-to-all-done = f32[4,256,1024]{2,1,0:T(8,128)} async-done(((f32[4,256,1024]{2,1,0:T(8,128)}), f32[4,256,1024]{2,1,0:T(8,128)}, u32[]{:S(2)}, u32[]{:S(2)}) %all-to-all-start) | async-done | bytes 4194336 | tf_op jit(solution)/shard_map/all_to_all | solution.py:23
  352.4 8.4 %fusion.86 = f32[1024,1024]{1,0:T(8,128)} fusion(f32[512,1024]{1,0:T(8,128)S(1)} %copy-done, f32[512,1024]{1,0:T(8,128)S(1)} %copy-done.3), kind=kOutput, calls=%fused_computation.180 | convolution fusion | flops 6442450944 | bytes 8388608 | tf_op jit(solution)/shard_map/dot_general | solution.py:38
  360.9 19.1 %collective-permute-done = f32[256,1024]{0,1:T(8,128)S(1)} collective-permute-done((f32[256,1024]{0,1:T(8,128)S(1)}, f32[256,1024]{0,1:T(8,128)S(1)}, u32[]{:S(2)}, u32[]{:S(2)}) %collective-permute-start) | collective-permute-done | bytes 1048608 | tf_op jit(solution)/shard_map/ppermute | solution.py:65
  384.4 44.2 %collective-permute-done.2 = f32[256,1024]{0,1:T(8,128)} collective-permute-done((f32[256,1024]{0,1:T(8,128)S(1)}, f32[256,1024]{0,1:T(8,128)}, u32[]{:S(2)}, u32[]{:S(2)}) %collective-permute-start.2) | collective-permute-done | bytes 1048608 | tf_op jit(solution)/shard_map/ppermute | solution.py:65
  430.9 5.6 copy.44
  436.5 4.4 fusion
  442.9 11.7 %cholesky.222 = f32[128,128]{1,0:T(8,128)S(1)} custom-call(f32[128,128]{1,0:T(8,128)S(1)} %cholesky.577), custom_call_target="Cholesky" | custom-call | tf_op jit(solution)/shard_map/jit(cholesky)/cholesky | solution.py:75
  454.8 9.8 %custom-call.62 = f32[1,128,128]{1,2,0:T(8,128)S(1)} custom-call(f32[1,128,128]{2,1,0:T(8,128)S(1)} %get-tuple-element.47), custom_call_target="InvertDiagBlocksLowerTriangular" | custom-call | tf_op jit(solution)/shard_map/jit(cholesky)/cholesky | solution.py:75
  467.9 11.7 %cholesky.243 = f32[128,128]{1,0:T(8,128)S(1)} custom-call(f32[128,128]{1,0:T(8,128)S(1)} %cholesky.581), custom_call_target="Cholesky" | custom-call | tf_op jit(solution)/shard_map/jit(cholesky)/cholesky | solution.py:75
  482.6 9.8 %custom-call.63 = f32[1,128,128]{1,2,0:T(8,128)S(1)} custom-call(f32[1,128,128]{2,1,0:T(8,128)S(1)} %get-tuple-element.45), custom_call_target="InvertDiagBlocksLowerTriangular" | custom-call | tf_op jit(solution)/shard_map/jit(cholesky)/cholesky | solution.py:75
  498.0 11.7 %cholesky.466 = f32[128,128]{1,0:T(8,128)S(1)} custom-call(f32[128,128]{1,0:T(8,128)S(1)} %cholesky.586), custom_call_target="Cholesky" | custom-call | tf_op jit(solution)/shard_map/jit(cholesky)/cholesky | solution.py:75
  509.8 9.8 %custom-call.64 = f32[1,128,128]{1,2,0:T(8,128)S(1)} custom-call(f32[1,128,128]{2,1,0:T(8,128)S(1)} %get-tuple-element.43), custom_call_target="InvertDiagBlocksLowerTriangular" | custom-call | tf_op jit(solution)/shard_map/jit(cholesky)/cholesky | solution.py:75
  521.5 3.3 slice_subtract_fusion.2
  524.8 11.7 %cholesky.485 = f32[128,128]{1,0:T(8,128)S(1)} custom-call(f32[128,128]{1,0:T(8,128)S(1)} %cholesky.591), custom_call_target="Cholesky" | custom-call | tf_op jit(solution)/shard_map/jit(cholesky)/cholesky | solution.py:75
  536.7 9.8 %custom-call.65 = f32[1,128,128]{1,2,0:T(8,128)S(1)} custom-call(f32[1,128,128]{2,1,0:T(8,128)S(1)} %get-tuple-element.41), custom_call_target="InvertDiagBlocksLowerTriangular" | custom-call | tf_op jit(solution)/shard_map/jit(cholesky)/cholesky | solution.py:75
  551.4 11.9 %cholesky.504 = f32[128,128]{1,0:T(8,128)S(1)} custom-call(f32[128,128]{1,0:T(8,128)S(1)} %cholesky.596), custom_call_target="Cholesky" | custom-call | tf_op jit(solution)/shard_map/jit(cholesky)/cholesky | solution.py:75
  563.4 9.8 %custom-call.66 = f32[1,128,128]{1,2,0:T(8,128)S(1)} custom-call(f32[1,128,128]{2,1,0:T(8,128)S(1)} %get-tuple-element.39), custom_call_target="InvertDiagBlocksLowerTriangular" | custom-call | tf_op jit(solution)/shard_map/jit(cholesky)/cholesky | solution.py:75
  575.0 3.2 slice_subtract_fusion.4
  578.3 11.7 %cholesky.524 = f32[128,128]{1,0:T(8,128)S(1)} custom-call(f32[128,128]{1,0:T(8,128)S(1)} %cholesky.601), custom_call_target="Cholesky" | custom-call | tf_op jit(solution)/shard_map/jit(cholesky)/cholesky | solution.py:75
  590.1 9.8 %custom-call.67 = f32[1,128,128]{1,2,0:T(8,128)S(1)} custom-call(f32[1,128,128]{2,1,0:T(8,128)S(1)} %get-tuple-element.37), custom_call_target="InvertDiagBlocksLowerTriangular" | custom-call | tf_op jit(solution)/shard_map/jit(cholesky)/cholesky | solution.py:75
  604.7 11.7 %cholesky.544 = f32[128,128]{1,0:T(8,128)S(1)} custom-call(f32[128,128]{1,0:T(8,128)S(1)} %cholesky.606), custom_call_target="Cholesky" | custom-call | tf_op jit(solution)/shard_map/jit(cholesky)/cholesky | solution.py:75
  616.6 9.8 %custom-call.68 = f32[1,128,128]{1,2,0:T(8,128)S(1)} custom-call(f32[1,128,128]{2,1,0:T(8,128)S(1)} %get-tuple-element.35), custom_call_target="InvertDiagBlocksLowerTriangular" | custom-call | tf_op jit(solution)/shard_map/jit(cholesky)/cholesky | solution.py:75
  630.2 11.7 %cholesky.562 = f32[128,128]{1,0:T(8,128)S(1)} custom-call(f32[128,128]{1,0:T(8,128)S(1)} %slice_subtract_fusion.6), custom_call_target="Cholesky" | custom-call | tf_op jit(solution)/shard_map/jit(cholesky)/cholesky | solution.py:75
  652.3 4.9 select_select_fusion
  659.6 28.3 %while.1 = (s32[]{:T(128)}, f32[1024,1024]{0,1:T(8,128)}, s32[8,2]{0,1:T(2,128)S(1)}, f32[8,128,128]{2,1,0:T(8,128)}, s32[]{:T(128)}) while((s32[]{:T(128)}, f32[1024,1024]{0,1:T(8,128)}, s32[8,2]{0,1:T(2,128)S(1)}, f32[8,128,128]{2,1,0:T(8,128)}, s32[]{:T(128)}) %tuple.39), condition=%wide.while_cond, body=%wide.while_body.sunk | while | flops 2 | bytes 393829 | solution.py:80
  688.0 79.4 %custom-call.69 = f32[8,128,128]{1,2,0:T(8,128)S(1)} custom-call(f32[8,128,128]{2,1,0:T(8,128)} %get-tuple-element.9), custom_call_target="InvertDiagBlocksLowerTriangular" | custom-call | tf_op jit(solution)/shard_map/triangular_solve | solution.py:80
  779.6 6.8 fusion.87
  (178 shorter events, 109.4 us)
Async XLA Ops:
  7.2 56.0 %all-gather.3.cloned.1.call-start = ((), (), s32[]{:S(2)}) async-start(), calls=%async_computation.2 | async-start | bytes 5242880 | tf_op jit(solution)/shard_map/all_gather | solution.py:48
  7.9 261.7 %all-reduce.3.cloned.1.call-start = ((), (), s32[]{:S(2)}) async-start(), calls=%async_computation.3 | async-start | bytes 6291456 | tf_op jit(solution)/shard_map/psum | solution.py:9
  274.3 3.1 copy-start.4
  287.3 55.0 %all-to-all-start = ((f32[4,256,1024]{2,1,0:T(8,128)}), f32[4,256,1024]{2,1,0:T(8,128)}, u32[]{:S(2)}, u32[]{:S(2)}) async-start(f32[4,256,1024]{2,1,0:T(8,128)} %fusion.85), calls=%async_computation | async-start | bytes 8388608 | tf_op jit(solution)/shard_map/all_to_all | solution.py:23
  292.2 365.1 %reduce-scatter.2.cloned.1.call-start = ((), (), s32[]{:S(2)}) async-start(), calls=%async_computation.4 | async-start | bytes 5242880 | tf_op jit(solution)/shard_map/reduce_scatter | solution.py:51
  345.3 7.1 copy-start
  345.4 7.1 copy-start.3
  349.2 30.8 %collective-permute-start = (f32[256,1024]{0,1:T(8,128)S(1)}, f32[256,1024]{0,1:T(8,128)S(1)}, u32[]{:S(2)}, u32[]{:S(2)}) collective-permute-start(f32[256,1024]{0,1:T(8,128)S(1)} %get-tuple-element.31), channel_id=1, source_target_pairs={{0,1},{1,2},{2,3},{3,0},{4,5},{5,6},{6,7},{7,4},{8,9},{9,10},{10,1... | collective-permute-start | bytes 3145736 | tf_op jit(solution)/shard_map/ppermute | solution.py:65
  349.8 32.2 %collective-permute-start.1 = (f32[256,1024]{0,1:T(8,128)S(1)}, f32[256,1024]{0,1:T(8,128)}, u32[]{:S(2)}, u32[]{:S(2)}) collective-permute-start(f32[256,1024]{0,1:T(8,128)S(1)} %get-tuple-element.31), channel_id=1, source_target_pairs={{0,3},{1,0},{2,1},{3,2},{4,7},{5,4},{6,5},{7,6},{8,11},{9,8},{10,9... | collective-permute-start | bytes 3145736 | tf_op jit(solution)/shard_map/ppermute | solution.py:70
  360.8 418.7 %all-gather.5.cloned.1.call-start = ((), (), s32[]{:S(2)}) async-start(), calls=%async_computation.5 | async-start | bytes 5242880 | tf_op jit(solution)/shard_map/all_gather | solution.py:83
  380.0 48.6 %collective-permute-start.2 = (f32[256,1024]{0,1:T(8,128)S(1)}, f32[256,1024]{0,1:T(8,128)}, u32[]{:S(2)}, u32[]{:S(2)}) collective-permute-start(f32[256,1024]{0,1:T(8,128)S(1)} %collective-permute-done), channel_id=1, source_target_pairs={{0,1},{1,2},{2,3},{3,0},{4,5},{5,6},{6,7},{7,4},{8,9},{9,10},{10,1... | collective-permute-start | bytes 3145736 | tf_op jit(solution)/shard_map/ppermute | solution.py:65
  440.9 2.0 copy-start.1
  652.3 5.0 copy-start.2
Sparse Core Ops, SparseCore 0:
  9.8 53.3 all-gather.2
  78.6 190.9 all-reduce.2
  360.9 72.0 reduce-scatter.1
  659.7 47.5 all-gather.4
